TPU v7x, 32 devices: a whole 2x2x4 slice. The times are simulated.
32 devices in a mesh: batch: 8 (over z, x), cols: 4 (over y, core).
Axes of the slice: x: 2, y: 2, z: 4, core: 2. Of those that a mesh axis runs over, the one named last changes fastest.
Arguments:
- partial_query: float32 [8, 1024, 1024], P('batch', None, 'cols'), may hold values from -0.875 to 0.875
- partial_key: float32 [8, 1024, 1024], P('batch', None, 'cols'), may hold values from -0.875 to 0.875
- partial_value: float32 [8, 1024, 1024], P('batch', None, 'cols'), may hold values from -0.875 to 0.875
- partial_mixed: float32 [8, 1024, 1024], P('batch', 'cols'), may hold values from -0.875 to 0.875
- partial_norm: float32 [8, 1024], P('batch'), may hold values from -8 to 8
- partial_bias: float32 [8, 1024], P('batch'), may hold values from -8 to 8
- master_query: float32 [1024, 1024], P('batch', 'cols'), may hold values from -0.1875 to 0.1875
- master_key: float32 [1024, 1024], P('batch', 'cols'), may hold values from -0.1875 to 0.1875
- master_value: float32 [1024, 1024], P('batch', 'cols'), may hold values from -0.1875 to 0.1875
- master_mixed: float32 [1024, 1024], P('cols', 'batch'), may hold values from -0.1875 to 0.1875
- master_norm: float32 [1024], P('batch'), may hold values from 0.25 to 1.75
- master_bias: float32 [1024], P('batch'), may hold values from -3 to 3
Outputs:
- compute_query: bfloat16 [1024, 1024], P(None, 'cols')
- compute_key: bfloat16 [1024, 1024], P(None, 'cols')
- compute_value: bfloat16 [1024, 1024], P(None, 'cols')
- compute_mixed: bfloat16 [1024, 1024], P('cols')
- compute_norm: bfloat16 [1024], replicated
- compute_bias: bfloat16 [1024], replicated
- stepped_query: float32 [1024, 1024], P('batch', 'cols')
- stepped_key: float32 [1024, 1024], P('batch', 'cols')
- stepped_value: float32 [1024, 1024], P('batch', 'cols')
- stepped_mixed: float32 [1024, 1024], P('cols', 'batch')
- stepped_norm: float32 [1024], P('batch')
- stepped_bias: float32 [1024], P('batch')
All inputs are finite; a program needn't handle non-finite values.
Results may differ from a plain program's by a relative error of at most 0.001.
Values may be sent and summed in bfloat16 or wider, within the bound.
A program may use at most 64 MiB of HBM per device.

v0:
```python
import jax
import jax.numpy as jnp
from jax import lax
from jax.sharding import PartitionSpec as P

learn_rate = 0.4


def per_device(
    partial_query,
    partial_key,
    partial_value,
    partial_mixed,
    partial_norm,
    partial_bias,
    master_query,
    master_key,
    master_value,
    master_mixed,
    master_norm,
    master_bias,
):
    mean_query, mean_key, mean_value, mean_mixed, mean_norm, mean_bias = (
        lax.psum_scatter(partial_query[0], "batch", scatter_dimension=0, tiled=True),
        lax.psum_scatter(partial_key[0], "batch", scatter_dimension=0, tiled=True),
        lax.psum_scatter(partial_value[0], "batch", scatter_dimension=0, tiled=True),
        lax.psum_scatter(partial_mixed[0], "batch", scatter_dimension=1, tiled=True),
        lax.psum_scatter(partial_norm[0], "batch", scatter_dimension=0, tiled=True),
        lax.psum_scatter(partial_bias[0], "batch", scatter_dimension=0, tiled=True),
    )
    mean_rate = lax.axis_size("batch") ** (-0.5)
    mean_query = mean_query * mean_rate
    mean_key = mean_key * mean_rate
    mean_value = mean_value * mean_rate
    mean_mixed = mean_mixed * mean_rate
    mean_norm = mean_norm * mean_rate
    mean_bias = mean_bias * mean_rate
    stepped_query = master_query - learn_rate * mean_query
    stepped_key = master_key - learn_rate * mean_key
    stepped_value = master_value - learn_rate * mean_value
    stepped_mixed = master_mixed - learn_rate * mean_mixed
    stepped_norm = master_norm - learn_rate * mean_norm
    stepped_bias = master_bias - learn_rate * mean_bias
    compute_query, compute_key, compute_value, compute_mixed, compute_norm, compute_bias = (
        lax.all_gather(stepped_query.astype(jnp.bfloat16), "batch", axis=0, tiled=True),
        lax.all_gather(stepped_key.astype(jnp.bfloat16), "batch", axis=0, tiled=True),
        lax.all_gather(stepped_value.astype(jnp.bfloat16), "batch", axis=0, tiled=True),
        lax.all_gather(stepped_mixed.astype(jnp.bfloat16), "batch", axis=1, tiled=True),
        lax.all_gather(stepped_norm.astype(jnp.bfloat16), "batch", axis=0, tiled=True),
        lax.all_gather(stepped_bias.astype(jnp.bfloat16), "batch", axis=0, tiled=True),
    )
    return (
        compute_query,
        compute_key,
        compute_value,
        compute_mixed,
        compute_norm,
        compute_bias,
        stepped_query,
        stepped_key,
        stepped_value,
        stepped_mixed,
        stepped_norm,
        stepped_bias,
    )


def solution(mesh):
    in_specs = (
        P("batch", None, "cols"),
        P("batch", None, "cols"),
        P("batch", None, "cols"),
        P("batch", "cols", None),
        P("batch", None),
        P("batch", None),
        P("batch", "cols"),
        P("batch", "cols"),
        P("batch", "cols"),
        P("cols", "batch"),
        P("batch"),
        P("batch"),
    )
    out_specs = (
        P(None, "cols"),
        P(None, "cols"),
        P(None, "cols"),
        P("cols", None),
        P(),
        P(),
        P("batch", "cols"),
        P("batch", "cols"),
        P("batch", "cols"),
        P("cols", "batch"),
        P("batch"),
        P("batch"),
    )
    return jax.shard_map(
        per_device, mesh=mesh, in_specs=in_specs, out_specs=out_specs, check_vma=False
    )
```

profile of v0, /device:TPU:0, one launch (start us, length us, event | category | flops | bytes accessed | tf_op | source)
XLA Modules:
  0.0 319.6 jit_solution(10118742841757105485)
XLA Ops:
  7.2 0.0 reduce-scatter.5.cloned.1.call-start
  7.2 0.7 reduce-scatter.5.cloned.1.call-update
  7.9 0.0 reduce-scatter.7.cloned.1.call-start
  8.0 0.7 reduce-scatter.7.cloned.1.call-update
  8.7 0.0 reduce-scatter.9.cloned.1.call-start
  8.7 0.7 reduce-scatter.9.cloned.1.call-update
  9.4 0.0 reduce-scatter.11.cloned.1.call-start
  9.4 0.0 copy-start
  9.5 0.5 reduce-scatter.11.cloned.1.call-update
  10.0 0.0 copy-start.8
  10.0 0.6 copy-done.8
  10.6 0.6 dynamic-slice
  11.2 0.0 copy-start.4
  11.2 0.0 copy-start.5
  11.9 0.0 copy-done.4
  11.9 0.0 copy-done.5
  11.9 23.6 %all-reduce.2 = (f32[1024]{0:T(1024)S(1)}, f32[1024]{0:T(1024)S(1)}) all-reduce(f32[1024]{0:T(1024)S(1)} %bitcast.17, f32[1024]{0:T(1024)S(1)} %bitcast.18), channel_id=6, replica_groups=mesh['batch'=8,'cols'=4] {'batch'}, use_global_device_ids=true, to_apply=%region_4.0.clone | all-reduce | flops 2048 | bytes 16384
  35.5 0.0 copy-start.6
  35.5 0.6 copy-done.6
  36.1 0.6 convert_bitcast_fusion.1
  36.7 16.3 %all-gather = bf16[8,1,128]{2,1,0:T(2,128)(2,1)S(1)} all-gather(bf16[1,1,128]{2,1,0:T(2,128)(2,1)S(1)} %get-tuple-element.16), channel_id=1, replica_groups=mesh['batch'=8,'cols'=4] {'batch'}, dimensions={0}, use_global_device_ids=true | all-gather | bytes 2304 | tf_op jit(solution)/shard_map/all_gather | solution.py:49
  53.0 0.6 reduce
  53.6 0.0 copy-start.7
  53.6 0.7 copy-done.7
  54.2 0.6 convert_bitcast_fusion
  54.8 18.4 %all-gather.1 = bf16[8,1,128]{2,1,0:T(2,128)(2,1)S(1)} all-gather(bf16[1,1,128]{2,1,0:T(2,128)(2,1)S(1)} %get-tuple-element.14), channel_id=1, replica_groups=mesh['batch'=8,'cols'=4] {'batch'}, dimensions={0}, use_global_device_ids=true | all-gather | bytes 2304 | tf_op jit(solution)/shard_map/all_gather | solution.py:50
  73.2 0.6 reduce.1
  73.8 5.2 %reduce-scatter.5.cloned.1.call-done = f32[128,256]{1,0:T(8,128)} async-done(((f32[1024,256]{1,0:T(8,128)}), f32[128,256]{1,0:T(8,128)}) %reduce-scatter.5.cloned.1.call-update) | async-done | bytes 131088 | tf_op jit(solution)/shard_map/reduce_scatter | solution.py:24
  79.0 0.0 copy-done
  79.0 1.6 fusion.7
  80.6 0.0 copy-start.1
  80.6 32.1 %all_gather.18 = bf16[1024,256]{1,0:T(8,128)(2,1)S(1)} all-gather(bf16[128,256]{1,0:T(8,128)(2,1)S(1)} %get-tuple-element.24), channel_id=1, replica_groups=mesh['batch'=8,'cols'=4] {'batch'}, dimensions={0}, use_global_device_ids=true | all-gather | bytes 589824 | tf_op jit(solution)/shard_map/all_gather | solution.py:45
  112.7 33.7 %reduce-scatter.7.cloned.1.call-done = f32[128,256]{1,0:T(8,128)} async-done(((f32[1024,256]{1,0:T(8,128)}), f32[128,256]{1,0:T(8,128)}) %reduce-scatter.7.cloned.1.call-update) | async-done | bytes 131088 | tf_op jit(solution)/shard_map/reduce_scatter | solution.py:25
  146.5 0.0 copy-done.1
  146.5 1.6 fusion.6
  148.1 32.5 %all_gather.19 = bf16[1024,256]{1,0:T(8,128)(2,1)S(1)} all-gather(bf16[128,256]{1,0:T(8,128)(2,1)S(1)} %get-tuple-element.22), channel_id=1, replica_groups=mesh['batch'=8,'cols'=4] {'batch'}, dimensions={0}, use_global_device_ids=true | all-gather | bytes 589824 | tf_op jit(solution)/shard_map/all_gather | solution.py:46
  180.5 33.4 %reduce-scatter.9.cloned.1.call-done = f32[128,256]{1,0:T(8,128)} async-done(((f32[1024,256]{1,0:T(8,128)}), f32[128,256]{1,0:T(8,128)}) %reduce-scatter.9.cloned.1.call-update) | async-done | bytes 131088 | tf_op jit(solution)/shard_map/reduce_scatter | solution.py:26
  213.9 0.0 copy-done.2
  213.9 1.6 fusion.5
  215.5 32.0 %all_gather.20 = bf16[1024,256]{1,0:T(8,128)(2,1)S(1)} all-gather(bf16[128,256]{1,0:T(8,128)(2,1)S(1)} %get-tuple-element.20), channel_id=1, replica_groups=mesh['batch'=8,'cols'=4] {'batch'}, dimensions={0}, use_global_device_ids=true | all-gather | bytes 589824 | tf_op jit(solution)/shard_map/all_gather | solution.py:47
  247.5 33.6 %reduce-scatter.11.cloned.1.call-done = f32[256,128]{1,0:T(8,128)} async-done(((f32[256,1024]{1,0:T(8,128)}), f32[256,128]{1,0:T(8,128)}) %reduce-scatter.11.cloned.1.call-update) | async-done | bytes 131088 | tf_op jit(solution)/shard_map/reduce_scatter | solution.py:27
  281.1 0.0 copy-done.3
  281.1 1.6 fusion.4
  282.7 27.2 %all_gather.21 = bf16[256,1024]{1,0:T(8,128)(2,1)S(1)} all-gather(bf16[256,128]{1,0:T(8,128)(2,1)S(1)} %get-tuple-element.18), channel_id=1, replica_groups=mesh['batch'=8,'cols'=4] {'batch'}, dimensions={1}, use_global_device_ids=true | all-gather | bytes 589824 | tf_op jit(solution)/shard_map/all_gather | solution.py:48
  309.9 0.8 copy.28
  310.7 0.8 copy.29
  311.5 0.8 copy.30
  312.3 0.8 copy.31
  (2 shorter events, 0.0 us)
Async XLA Ops:
  7.2 71.9 %reduce-scatter.5.cloned.1.call-start = ((), (), s32[]{:S(2)}) async-start(), calls=%async_computation.4 | async-start | bytes 1179648 | tf_op jit(solution)/shard_map/reduce_scatter | solution.py:24
  7.9 138.6 %reduce-scatter.7.cloned.1.call-start = ((), (), s32[]{:S(2)}) async-start(), calls=%async_computation.5 | async-start | bytes 1179648 | tf_op jit(solution)/shard_map/reduce_scatter | solution.py:25
  8.7 205.2 %reduce-scatter.9.cloned.1.call-start = ((), (), s32[]{:S(2)}) async-start(), calls=%async_computation.6 | async-start | bytes 1179648 | tf_op jit(solution)/shard_map/reduce_scatter | solution.py:26
  9.4 271.7 %reduce-scatter.11.cloned.1.call-start = ((), (), s32[]{:S(2)}) async-start(), calls=%async_computation.7 | async-start | bytes 1179648 | tf_op jit(solution)/shard_map/reduce_scatter | solution.py:27
  9.4 69.6 %copy-start = (f32[128,256]{1,0:T(8,128)S(1)}, f32[128,256]{1,0:T(8,128)}, u32[]{:S(2)}) copy-start(f32[128,256]{1,0:T(8,128)} %param.18) | copy-start | bytes 393220
  10.0 0.7 copy-start.8
  11.2 0.7 copy-start.4
  11.2 0.7 copy-start.5
  35.5 0.7 copy-start.6
  53.6 0.7 copy-start.7
  80.6 65.9 %copy-start.1 = (f32[128,256]{1,0:T(8,128)S(1)}, f32[128,256]{1,0:T(8,128)}, u32[]{:S(2)}) copy-start(f32[128,256]{1,0:T(8,128)} %param.19) | copy-start | bytes 393220
  148.0 65.8 %copy-start.2 = (f32[128,256]{1,0:T(8,128)S(1)}, f32[128,256]{1,0:T(8,128)}, u32[]{:S(2)}) copy-start(f32[128,256]{1,0:T(8,128)} %param.20) | copy-start | bytes 393220
  215.5 65.7 %copy-start.3 = (f32[256,128]{1,0:T(8,128)S(1)}, f32[256,128]{1,0:T(8,128)}, u32[]{:S(2)}) copy-start(f32[256,128]{1,0:T(8,128)} %param.21) | copy-start | bytes 393220
Sparse Core Ops, SparseCore 0:
  11.4 67.5 reduce-scatter.4
  82.4 63.9 reduce-scatter.6
  149.9 63.9 reduce-scatter.8
  217.1 63.9 reduce-scatter.10
where the time goes:
time: 320 us
  blocking collectives  182 us (57%)
  waiting for transfers between devices  109 us (34%)
  between operations  14.5 us (5%)
  other arithmetic  8.68 us (3%)
  local copies, waits for them, and re-layouts  5.74 us (2%)
    reduce_scatter x1, waiting for transfers between devices, per_device(): lax.psum_scatter(partial_key[0], 'batch', scatter_dimension=0, tiled=True)  33.7 us
    reduce_scatter x1, waiting for transfers between devices, per_device(): lax.psum_scatter(partial_mixed[0], 'batch', scatter_dimension=1, tiled=True)  33.6 us
    reduce_scatter x1, waiting for transfers between devices, per_device(): lax.psum_scatter(partial_value[0], 'batch', scatter_dimension=0, tiled=True)  33.4 us
    all_gather x1, blocking collectives, per_device(): lax.all_gather(stepped_key.astype(jnp.bfloat16), 'batch', axis=0, tiled=T...  32.5 us
    all_gather x1, blocking collectives, per_device(): lax.all_gather(stepped_query.astype(jnp.bfloat16), 'batch', axis=0, tiled...  32.1 us
    all_gather x1, blocking collectives, per_device(): lax.all_gather(stepped_value.astype(jnp.bfloat16), 'batch', axis=0, tiled...  32 us
    all_gather x1, blocking collectives, per_device(): lax.all_gather(stepped_mixed.astype(jnp.bfloat16), 'batch', axis=1, tiled...  27.2 us
    unnamed x1, blocking collectives  23.6 us
  transfers between devices with their start and end apart: 4, of which 4 were waited for; matrix products, arithmetic and copies ran while one was open for 2% of the time, Pallas kernels for 0%

commit v1 on v0

v1 whole, which is shorter than its diff:
```python
import functools

import jax
import jax.numpy as jnp
from jax import lax
from jax.experimental import pallas as pl
from jax.experimental.pallas import tpu as pltpu
from jax.sharding import PartitionSpec as P

learn_rate = 0.4
HALVES = 2
SPAN = 118.0


def encode(x, limit):
    power = jnp.exp2(jnp.abs(x) * (2 * SPAN / limit) - SPAN)
    return jnp.where(x < 0, -power, power).astype(jnp.bfloat16)


def decode(code, limit):
    y = code.astype(jnp.float32)
    size = (jnp.log2(jnp.abs(y)) + SPAN) * (limit / (2 * SPAN))
    return jnp.where(y < 0, -size, size)


def kernel(n, kinds, limit, *refs):
    count = len(kinds)
    groups = n // 2
    refs = list(refs)

    def take(k):
        out = refs[:k]
        del refs[:k]
        return out

    partial, master = take(count), take(count)
    norm, bias, norm_master, bias_master = take(4)
    gathered, stepped = take(count), take(count)
    vec_all, vec_mine = take(2)
    pair_out, pair_in, part_out, part_in = take(count), take(count), take(count), take(count)
    own, vec_out, vec_in = take(count), *[take(1)[0] for _ in range(2)]
    a_send, a_recv, b_send, b_recv, c_send, c_recv, d_send, d_recv = take(8)
    v_send, v_recv, w_send, w_recv = take(4)

    rate = n ** (-0.5)
    b = lax.axis_index("batch")
    side = lax.rem(b, 2)
    g = b // 2
    partner = b + 1 - 2 * side

    def remote(src, dst, send, recv, to):
        return pltpu.make_async_remote_copy(
            src_ref=src,
            dst_ref=dst,
            send_sem=send,
            recv_sem=recv,
            device_id={"batch": to},
            device_id_type=pl.DeviceIdType.MESH,
        )

    chunks = [(a, h) for h in range(HALVES) for a in range(count)]

    def place(a, h, d):
        rows, cols = stepped[a].shape
        r = rows // HALVES
        if kinds[a] == "rows":
            return pl.ds(pl.multiple_of(d * rows + h * r, r), r), pl.ds(0, cols)
        return pl.ds(h * r, r), pl.ds(pl.multiple_of(d * cols, cols), cols)

    def load(a, h, d):
        rows, cols = place(a, h, d)
        return partial[a][0, rows, cols]

    def other(k):
        return lax.rem(g + k, groups)

    barrier = pltpu.get_barrier_semaphore()
    for k in range(1, n):
        pl.semaphore_signal(
            barrier,
            inc=1,
            device_id={"batch": lax.rem(b + k, n)},
            device_id_type=pl.DeviceIdType.MESH,
        )

    def pair_encode(c):
        a, h = chunks[c]

        def body(k, carry):
            pair_out[a][h, k] = encode(load(a, h, 2 * k + 1 - side), limit)
            return carry

        lax.fori_loop(0, groups, body, 0)

    def pair_copy(c):
        a, h = chunks[c]
        return remote(
            pair_out[a].at[h], pair_in[a].at[h], a_send.at[c], a_recv.at[c], partner
        )

    def part_copy(c, src_slot, dst_slot, to):
        a, h = chunks[c]
        return remote(
            part_out[a].at[h, src_slot],
            part_in[a].at[h, dst_slot],
            b_send.at[c, src_slot],
            b_recv.at[c, dst_slot],
            2 * to + side,
        )

    def pair_finish(c):
        a, h = chunks[c]
        pair_copy(c).wait_recv()
        for k in range(1, groups):
            to = other(k)
            total = load(a, h, 2 * to + side) + decode(pair_in[a][h, to], limit)
            part_out[a][h, to] = encode(total, 2 * limit)
            part_copy(c, to, g, to).start()
        own[a][h] = load(a, h, b) + decode(pair_in[a][h, g], limit)

    def back_copy(c, owner, slot, to):
        a, h = chunks[c]
        rows, cols = place(a, h, owner)
        block = gathered[a].at[rows, cols]
        return remote(block, block, c_send.at[c, slot], c_recv.at[c, owner // 2], to)

    def cross_copy(c, owner, recv_owner):
        a, h = chunks[c]
        rows, cols = place(a, h, owner)
        block = gathered[a].at[rows, cols]
        return remote(
            block, block, d_send.at[c, owner // 2], d_recv.at[c, recv_owner // 2], partner
        )

    def part_finish(c):
        a, h = chunks[c]
        r = stepped[a].shape[0] // HALVES
        total = own[a][h]
        for k in range(1, groups):
            source = other(k)
            part_copy(c, source, source, source).wait_recv()
            total = total + decode(part_in[a][h, source], 2 * limit)
        rows = pl.ds(h * r, r)
        new = master[a][rows, :] - learn_rate * (total * rate)
        stepped[a][rows, :] = new
        at_rows, at_cols = place(a, h, b)
        gathered[a][at_rows, at_cols] = new.astype(jnp.bfloat16)
        for k in range(1, groups):
            back_copy(c, b, k, 2 * other(k) + side).start()
        cross_copy(c, b, b).start()

    def cross_finish(c):
        for k in range(1, groups):
            owner = 2 * other(k) + side
            back_copy(c, owner, k, owner).wait_recv()
            cross_copy(c, owner, owner).start()

    def vec_copy(k):
        to = lax.rem(b + k, n)
        return remote(vec_out.at[to], vec_in.at[b], v_send.at[to], v_recv.at[b], to)

    def vec_back(k):
        to = lax.rem(b + k, n)
        return remote(vec_all.at[b], vec_all.at[b], w_send.at[to], w_recv.at[b], to)

    pair_encode(0)
    pl.semaphore_wait(barrier, n - 1)
    pair_copy(0).start()
    for d in range(n):
        vec_out[d, 0:1, :] = norm[d]
        vec_out[d, 1:2, :] = bias[d]
    for k in range(1, n):
        vec_copy(k).start()
    for c in range(1, len(chunks)):
        pair_encode(c)
        pair_copy(c).start()

    for t in range(len(chunks) + 2):
        if t < len(chunks):
            pair_finish(t)
        if 0 <= t - 1 < len(chunks):
            part_finish(t - 1)
        if t == 1:
            total = vec_out[b]
            for k in range(1, n):
                source = lax.rem(b + k, n)
                remote(
                    vec_out.at[source],
                    vec_in.at[source],
                    v_send.at[source],
                    v_recv.at[source],
                    source,
                ).wait_recv()
                total = total + vec_in[source]
            mean = total * rate
            vec_mine[0:1, :] = norm_master[...] - learn_rate * mean[0:1]
            vec_mine[1:2, :] = bias_master[...] - learn_rate * mean[1:2]
            vec_all[b] = vec_mine[...]
            for k in range(1, n):
                vec_back(k).start()
        if 0 <= t - 2 < len(chunks):
            cross_finish(t - 2)

    for c in range(len(chunks)):
        for k in range(groups):
            owner = 2 * other(k) + 1 - side
            cross_copy(c, owner, owner).wait_recv()
    for k in range(1, n):
        source = lax.rem(b + k, n)
        remote(
            vec_all.at[source],
            vec_all.at[source],
            w_send.at[source],
            w_recv.at[source],
            source,
        ).wait_recv()
    for k in range(1, n):
        vec_copy(k).wait_send()
        vec_back(k).wait_send()
    for c in range(len(chunks)):
        pair_copy(c).wait_send()
        for k in range(1, groups):
            to = other(k)
            part_copy(c, to, g, to).wait_send()
            back_copy(c, b, k, 2 * to + side).wait_send()
        for k in range(groups):
            owner = 2 * other(k) + side
            cross_copy(c, owner, owner).wait_send()


def per_device(
    partial_query,
    partial_key,
    partial_value,
    partial_mixed,
    partial_norm,
    partial_bias,
    master_query,
    master_key,
    master_value,
    master_mixed,
    master_norm,
    master_bias,
):
    n = lax.axis_size("batch")
    groups = n // 2
    limit = 0.875 if n <= 8 else 1.25
    wide = master_mixed.shape[1] % 128 == 0
    kinds = ("rows", "rows", "rows", "cols" if wide else "rows")
    if not wide:
        partial_mixed = jnp.swapaxes(partial_mixed, 1, 2)
        master_mixed = master_mixed.T
    partials = (partial_query, partial_key, partial_value, partial_mixed)
    masters = (master_query, master_key, master_value, master_mixed)
    chunk_count = len(partials) * HALVES
    w = master_norm.shape[0]

    out_shape = [jax.ShapeDtypeStruct(p.shape[1:], jnp.bfloat16) for p in partials]
    out_shape += [jax.ShapeDtypeStruct(m.shape, jnp.float32) for m in masters]
    out_shape += [
        jax.ShapeDtypeStruct((n, 2, w), jnp.float32),
        jax.ShapeDtypeStruct((2, w), jnp.float32),
    ]
    coded = [
        pltpu.VMEM((HALVES, groups, m.shape[0] // HALVES, m.shape[1]), jnp.bfloat16)
        for m in masters
    ]
    owns = [
        pltpu.VMEM((HALVES, m.shape[0] // HALVES, m.shape[1]), jnp.float32)
        for m in masters
    ]
    dma = pltpu.SemaphoreType.DMA
    vmem = pl.BlockSpec(memory_space=pltpu.VMEM)
    outs = pl.pallas_call(
        functools.partial(kernel, n, kinds, limit),
        out_shape=out_shape,
        in_specs=[vmem] * (2 * len(partials) + 4),
        out_specs=[vmem] * len(out_shape),
        scratch_shapes=coded * 4
        + owns
        + [pltpu.VMEM((n, 2, w), jnp.float32)] * 2
        + [dma((chunk_count,))] * 2
        + [dma((chunk_count, groups))] * 6
        + [dma((n,))] * 4,
        compiler_params=pltpu.CompilerParams(collective_id=0, has_side_effects=True),
    )(
        *partials,
        *masters,
        partial_norm.reshape(n, 1, w),
        partial_bias.reshape(n, 1, w),
        master_norm.reshape(1, w),
        master_bias.reshape(1, w),
    )
    computes, steppeds, (vec_all, vec_mine) = outs[:4], outs[4:8], outs[8:]
    if not wide:
        computes = (*computes[:3], computes[3].T)
        steppeds = (*steppeds[:3], steppeds[3].T)
    vec_low = vec_all.astype(jnp.bfloat16)
    return (
        *computes,
        vec_low[:, 0].reshape(-1),
        vec_low[:, 1].reshape(-1),
        *steppeds,
        vec_mine[0],
        vec_mine[1],
    )


def solution(mesh):
    in_specs = (
        P("batch", None, "cols"),
        P("batch", None, "cols"),
        P("batch", None, "cols"),
        P("batch", "cols", None),
        P("batch", None),
        P("batch", None),
        P("batch", "cols"),
        P("batch", "cols"),
        P("batch", "cols"),
        P("cols", "batch"),
        P("batch"),
        P("batch"),
    )
    out_specs = (
        P(None, "cols"),
        P(None, "cols"),
        P(None, "cols"),
        P("cols", None),
        P(),
        P(),
        P("batch", "cols"),
        P("batch", "cols"),
        P("batch", "cols"),
        P("cols", "batch"),
        P("batch"),
        P("batch"),
    )
    return jax.shard_map(
        per_device, mesh=mesh, in_specs=in_specs, out_specs=out_specs, check_vma=False
    )
```

time: 320 us -> 80.6 us (0.25)
  blocking collectives: 182 us -> 0 us
  waiting for transfers between devices: 109 us -> 0 us
  Pallas kernels: 0 us -> 68.1 us
  between operations: 14.5 us -> 0.67 us
  other arithmetic: 8.68 us -> 0.7 us
  local copies, waits for them, and re-layouts: 5.74 us -> 10.7 us
    all_gather x6 -> x0, blocking collectives: 158 us -> none  [the longest x1 32.5 us: per_device(): lax.all_gather(stepped_key.astype(jnp.bfloat16), 'batch', axis=0, tiled=T...]
    reduce_scatter x4 -> x0, waiting for transfers between devices: 106 us -> none  [the longest x1 33.7 us: per_device(): lax.psum_scatter(partial_key[0], 'batch', scatter_dimension=0, tiled=True)]
    pallas_call x0 -> x1, Pallas kernels: none -> 68.1 us  [per_device(): pl.pallas_call(functools.partial(kernel, n, kinds, limit), out_shape=out_...]
    unnamed x1 -> x0, blocking collectives: 23.6 us -> none
    convert_element_type x4 -> x1, other arithmetic: 6.31 us -> 0.7 us  [per_device(): vec_low = vec_all.astype(jnp.bfloat16)]
    unnamed x23 -> x24, local copies, waits for them, and re-layouts: 5.74 us -> 9.59 us
  transfers between devices with their start and end apart: 4 -> 0, of which waited for: 4 -> 0; matrix products, arithmetic and copies ran while one was open for 2% -> 0% of each run, Pallas kernels for 0% -> 0%
where the time goes in v1:
time: 80.6 us; the launch traced here: 80.2 us
  Pallas kernels  68.1 us (84%)
  local copies, waits for them, and re-layouts  10.7 us (13%)
    pallas_call x1, Pallas kernels, per_device(): pl.pallas_call(functools.partial(kernel, n, kinds, limit), out_shape=out_...  68.1 us
    unnamed x24, local copies, waits for them, and re-layouts  9.59 us

profile of v1, /device:TPU:0, one launch (start us, length us, event | category | flops | bytes accessed | tf_op | source)
XLA Modules:
  0.0 80.2 jit_solution(17891226878041283013)
XLA Ops:
  0.6 68.1 %shard_map.211 = (bf16[1024,256]{1,0:T(8,128)(2,1)}, bf16[1024,256]{1,0:T(8,128)(2,1)}, bf16[1024,256]{1,0:T(8,128)(2,1)}, bf16[256,1024]{1,0:T(8,128)(2,1)}, f3...) custom-call(f32[1,1024,256]{2,1,0:T(8,128)} %refs_0_.1, ...), custom_call_target="tpu_custom_call" | custom-call | tf_op jit(solution)/shard_map/pallas_call | solution.py:274
  68.8 0.7 convert_element_type.3
  69.5 0.6 slice_reduce_fusion
  70.1 0.0 copy-start.7
  70.1 0.7 copy-done.7
  70.8 0.5 slice_bitcast_fusion
  71.3 0.0 copy-start.2
  71.3 1.9 %copy.32 = bf16[1024,256]{1,0:T(8,128)(2,1)} copy(bf16[1024,256]{1,0:T(8,128)(2,1)} %get-tuple-element.48) | data formatting | bytes 1048576
  73.2 0.0 copy-done.2
  73.2 0.0 copy-start.1
  73.2 0.8 copy.33
  74.0 0.4 copy-done.1
  74.5 0.0 copy-start
  74.5 0.8 copy.34
  75.3 0.4 copy-done
  75.7 0.0 copy-start.6
  75.7 0.8 copy.35
  76.5 0.2 copy-done.6
  76.7 0.0 copy-start.5
  76.7 0.7 copy.36
  77.4 0.3 copy-done.5
  77.7 0.0 copy-start.4
  77.7 0.7 copy.37
  78.3 0.3 copy-done.4
  78.6 0.0 copy-start.3
  78.6 0.7 copy.38
  79.3 0.3 copy-done.3
  79.6 0.7 copy.39
Async XLA Ops:
  70.1 0.7 copy-start.7
  71.3 1.9 %copy-start.2 = (bf16[1024,256]{1,0:T(8,128)(2,1)S(1)}, bf16[1024,256]{1,0:T(8,128)(2,1)}, u32[]{:S(2)}) copy-start(bf16[1024,256]{1,0:T(8,128)(2,1)} %get-tuple-element.49) | copy-start | bytes 1572868
  73.2 1.2 %copy-start.1 = (bf16[1024,256]{1,0:T(8,128)(2,1)S(1)}, bf16[1024,256]{1,0:T(8,128)(2,1)}, u32[]{:S(2)}) copy-start(bf16[1024,256]{1,0:T(8,128)(2,1)} %get-tuple-element.50) | copy-start | bytes 1572868
  74.5 1.2 %copy-start = (bf16[256,1024]{1,0:T(8,128)(2,1)S(1)}, bf16[256,1024]{1,0:T(8,128)(2,1)}, u32[]{:S(2)}) copy-start(bf16[256,1024]{1,0:T(8,128)(2,1)} %get-tuple-element.51) | copy-start | bytes 1572868
  75.7 1.0 %copy-start.6 = (f32[128,256]{1,0:T(8,128)S(1)}, f32[128,256]{1,0:T(8,128)}, u32[]{:S(2)}) copy-start(f32[128,256]{1,0:T(8,128)} %get-tuple-element.54) | copy-start | bytes 393220
  76.7 1.0 %copy-start.5 = (f32[128,256]{1,0:T(8,128)S(1)}, f32[128,256]{1,0:T(8,128)}, u32[]{:S(2)}) copy-start(f32[128,256]{1,0:T(8,128)} %get-tuple-element.55) | copy-start | bytes 393220
  77.7 1.0 %copy-start.4 = (f32[128,256]{1,0:T(8,128)S(1)}, f32[128,256]{1,0:T(8,128)}, u32[]{:S(2)}) copy-start(f32[128,256]{1,0:T(8,128)} %get-tuple-element.56) | copy-start | bytes 393220
  78.6 1.0 %copy-start.3 = (f32[256,128]{1,0:T(8,128)S(1)}, f32[256,128]{1,0:T(8,128)}, u32[]{:S(2)}) copy-start(f32[256,128]{1,0:T(8,128)} %get-tuple-element.57) | copy-start | bytes 393220

commit v2 on v1

--- a/solution.py
+++ b/solution.py
@@ -33,12 +33,14 @@
         del refs[:k]
         return out
 
-    partial, master = take(count), take(count)
+    source, master = take(count), take(count)
     norm, bias, norm_master, bias_master = take(4)
     gathered, stepped = take(count), take(count)
     vec_all, vec_mine = take(2)
     pair_out, pair_in, part_out, part_in = take(count), take(count), take(count), take(count)
-    own, vec_out, vec_in = take(count), *[take(1)[0] for _ in range(2)]
+    own, partial = take(count), take(count)
+    vec_out, vec_in = take(2)
+    (in_sem,) = take(1)
     a_send, a_recv, b_send, b_recv, c_send, c_recv, d_send, d_recv = take(8)
     v_send, v_recv, w_send, w_recv = take(4)
 
@@ -69,10 +71,17 @@
 
     def load(a, h, d):
         rows, cols = place(a, h, d)
-        return partial[a][0, rows, cols]
+        return partial[a][rows, cols]
 
     def other(k):
         return lax.rem(g + k, groups)
+
+    loads = [
+        pltpu.make_async_copy(source[a].at[0], partial[a], in_sem.at[a])
+        for a in range(count)
+    ]
+    for copy in loads:
+        copy.start()
 
     barrier = pltpu.get_barrier_semaphore()
     for k in range(1, n):
@@ -118,11 +127,23 @@
             part_copy(c, to, g, to).start()
         own[a][h] = load(a, h, b) + decode(pair_in[a][h, g], limit)
 
-    def back_copy(c, owner, slot, to):
+    def line_copy(c, owner, way, to=None):
         a, h = chunks[c]
         rows, cols = place(a, h, owner)
         block = gathered[a].at[rows, cols]
-        return remote(block, block, c_send.at[c, slot], c_recv.at[c, owner // 2], to)
+        return remote(
+            block,
+            block,
+            c_send.at[(way + 1) // 2, c, owner // 2],
+            c_recv.at[c, owner // 2],
+            b + 2 * way if to is None else to,
+        )
+
+    def has_next(way):
+        return g < groups - 1 if way > 0 else g > 0
+
+    def has_source(way, k):
+        return g - k >= 0 if way > 0 else g + k < groups
 
     def cross_copy(c, owner, recv_owner):
         a, h = chunks[c]
@@ -145,15 +166,27 @@
         stepped[a][rows, :] = new
         at_rows, at_cols = place(a, h, b)
         gathered[a][at_rows, at_cols] = new.astype(jnp.bfloat16)
-        for k in range(1, groups):
-            back_copy(c, b, k, 2 * other(k) + side).start()
+        for way in (1, -1):
+
+            @pl.when(has_next(way))
+            def _():
+                line_copy(c, b, way).start()
+
         cross_copy(c, b, b).start()
 
-    def cross_finish(c):
-        for k in range(1, groups):
-            owner = 2 * other(k) + side
-            back_copy(c, owner, k, owner).wait_recv()
-            cross_copy(c, owner, owner).start()
+    def line_finish(c, k):
+        for way in (1, -1):
+
+            @pl.when(has_source(way, k))
+            def _():
+                owner = b - 2 * k * way
+                line_copy(c, owner, way, owner).wait_recv()
+
+                @pl.when(has_next(way))
+                def _():
+                    line_copy(c, owner, way).start()
+
+                cross_copy(c, owner, owner).start()
 
     def vec_copy(k):
         to = lax.rem(b + k, n)
@@ -163,6 +196,7 @@
         to = lax.rem(b + k, n)
         return remote(vec_all.at[b], vec_all.at[b], w_send.at[to], w_recv.at[b], to)
 
+    loads[0].wait()
     pair_encode(0)
     pl.semaphore_wait(barrier, n - 1)
     pair_copy(0).start()
@@ -172,10 +206,12 @@
     for k in range(1, n):
         vec_copy(k).start()
     for c in range(1, len(chunks)):
+        if c < count:
+            loads[c].wait()
         pair_encode(c)
         pair_copy(c).start()
 
-    for t in range(len(chunks) + 2):
+    for t in range(len(chunks) + groups):
         if t < len(chunks):
             pair_finish(t)
         if 0 <= t - 1 < len(chunks):
@@ -198,8 +234,9 @@
             vec_all[b] = vec_mine[...]
             for k in range(1, n):
                 vec_back(k).start()
-        if 0 <= t - 2 < len(chunks):
-            cross_finish(t - 2)
+        for k in range(groups - 1, 0, -1):
+            if 0 <= t - 1 - k < len(chunks):
+                line_finish(t - 1 - k, k)
 
     for c in range(len(chunks)):
         for k in range(groups):
@@ -222,10 +259,45 @@
         for k in range(1, groups):
             to = other(k)
             part_copy(c, to, g, to).wait_send()
-            back_copy(c, b, k, 2 * to + side).wait_send()
         for k in range(groups):
             owner = 2 * other(k) + side
             cross_copy(c, owner, owner).wait_send()
+        for way in (1, -1):
+
+            @pl.when(has_next(way))
+            def _():
+                line_copy(c, b, way).wait_send()
+
+            for k in range(1, groups):
+
+                @pl.when(has_source(way, k) & has_next(way))
+                def _():
+                    line_copy(c, b - 2 * k * way, way).wait_send()
+
+
+def hand_over(count, *refs):
+    sources, vec_all, vec_mine = refs[:count], refs[count], refs[count + 1]
+    targets = refs[count + 2 : 2 * count + 2]
+    norm, bias, norm_step, bias_step = refs[2 * count + 2 : 2 * count + 6]
+    held = refs[2 * count + 6 : 3 * count + 6]
+    in_sem, out_sem = refs[3 * count + 6 :]
+    ins = [
+        pltpu.make_async_copy(sources[i], held[i], in_sem.at[i]) for i in range(count)
+    ]
+    outs = [
+        pltpu.make_async_copy(held[i], targets[i], out_sem.at[i]) for i in range(count)
+    ]
+    for copy in ins:
+        copy.start()
+    norm[...] = vec_all[:, 0, :].astype(jnp.bfloat16)
+    bias[...] = vec_all[:, 1, :].astype(jnp.bfloat16)
+    norm_step[...] = vec_mine[0:1, :]
+    bias_step[...] = vec_mine[1:2, :]
+    for i in range(count):
+        ins[i].wait()
+        outs[i].start()
+    for copy in outs:
+        copy.wait()
 
 
 def per_device(
@@ -271,16 +343,21 @@
     ]
     dma = pltpu.SemaphoreType.DMA
     vmem = pl.BlockSpec(memory_space=pltpu.VMEM)
+    hbm = pl.BlockSpec(memory_space=pltpu.HBM)
     outs = pl.pallas_call(
         functools.partial(kernel, n, kinds, limit),
         out_shape=out_shape,
-        in_specs=[vmem] * (2 * len(partials) + 4),
+        in_specs=[hbm] * len(partials) + [vmem] * (len(partials) + 4),
         out_specs=[vmem] * len(out_shape),
         scratch_shapes=coded * 4
         + owns
+        + [pltpu.VMEM(p.shape[1:], jnp.float32) for p in partials]
         + [pltpu.VMEM((n, 2, w), jnp.float32)] * 2
+        + [dma((len(partials),))]
         + [dma((chunk_count,))] * 2
-        + [dma((chunk_count, groups))] * 6
+        + [dma((chunk_count, groups))] * 2
+        + [dma((2, chunk_count, groups))]
+        + [dma((chunk_count, groups))] * 3
         + [dma((n,))] * 4,
         compiler_params=pltpu.CompilerParams(collective_id=0, has_side_effects=True),
     )(
@@ -291,19 +368,24 @@
         master_norm.reshape(1, w),
         master_bias.reshape(1, w),
     )
-    computes, steppeds, (vec_all, vec_mine) = outs[:4], outs[4:8], outs[8:]
+    large, (vec_all, vec_mine) = outs[:8], outs[8:]
+    tail_shape = [jax.ShapeDtypeStruct(x.shape, x.dtype) for x in large]
+    tail_shape += [jax.ShapeDtypeStruct((n, w), jnp.bfloat16)] * 2
+    tail_shape += [jax.ShapeDtypeStruct((1, w), jnp.float32)] * 2
+    outs = pl.pallas_call(
+        functools.partial(hand_over, len(large)),
+        out_shape=tail_shape,
+        in_specs=[hbm] * len(large) + [vmem] * 2,
+        out_specs=[hbm] * len(large) + [vmem] * 4,
+        scratch_shapes=[pltpu.VMEM(x.shape, x.dtype) for x in large]
+        + [dma((len(large),))] * 2,
+    )(*large, vec_all, vec_mine)
+    computes, steppeds, vectors = outs[:4], outs[4:8], outs[8:]
     if not wide:
         computes = (*computes[:3], computes[3].T)
         steppeds = (*steppeds[:3], steppeds[3].T)
-    vec_low = vec_all.astype(jnp.bfloat16)
-    return (
-        *computes,
-        vec_low[:, 0].reshape(-1),
-        vec_low[:, 1].reshape(-1),
-        *steppeds,
-        vec_mine[0],
-        vec_mine[1],
-    )
+    norm, bias, norm_step, bias_step = (v.reshape(-1) for v in vectors)
+    return (*computes, norm, bias, *steppeds, norm_step, bias_step)
 
 
 def solution(mesh):

time: 80.6 us -> 66.9 us (0.83)
  local copies, waits for them, and re-layouts: 10.7 us -> 0 us
  Pallas kernels: 68.1 us -> 66 us
    unnamed x24 -> x0, local copies, waits for them, and re-layouts: 9.59 us -> none
    pallas_call x1, Pallas kernels: 68.1 us -> 62 us  [per_device(): pl.pallas_call(functools.partial(kernel, n, kinds, limit), out_shape=out_...]
    pallas_call x0 -> x1, Pallas kernels: none -> 3.95 us  [per_device(): pl.pallas_call(functools.partial(hand_over, len(large)), out_shape=tail_s...]
where the time goes in v2:
time: 66.9 us; the launch traced here: 66.6 us
  Pallas kernels  66 us (99%)
    pallas_call x1, Pallas kernels, per_device(): pl.pallas_call(functools.partial(kernel, n, kinds, limit), out_shape=out_...  62 us
    pallas_call x1, Pallas kernels, per_device(): pl.pallas_call(functools.partial(hand_over, len(large)), out_shape=tail_s...  3.95 us

profile of v2, /device:TPU:0, one launch (start us, length us, event | category | flops | bytes accessed | tf_op | source)
XLA Modules:
  0.0 66.6 jit_solution(16126031741940400865)
XLA Ops:
  0.6 62.0 %shard_map.211 = (bf16[1024,256]{1,0:T(8,128)(2,1)}, bf16[1024,256]{1,0:T(8,128)(2,1)}, bf16[1024,256]{1,0:T(8,128)(2,1)}, bf16[256,1024]{1,0:T(8,128)(2,1)}, f3...) custom-call(f32[1,1024,256]{2,1,0:T(8,128)} %refs_0_.1, ...), custom_call_target="tpu_custom_call" | custom-call | tf_op jit(solution)/shard_map/pallas_call | solution.py:347
  62.7 4.0 %shard_map.212 = (bf16[1024,256]{1,0:T(8,128)(2,1)}, bf16[1024,256]{1,0:T(8,128)(2,1)}, bf16[1024,256]{1,0:T(8,128)(2,1)}, bf16[256,1024]{1,0:T(8,128)(2,1)}, f3...) custom-call(bf16[1024,256]{1,0:T(8,128)(2,1)} %get-tuple-element.34., ...), custom_call_target="tpu_custom_call" | custom-call | tf_op jit(solution)/shard_map/pallas_call | solution.py:375

commit v3 on v2

--- a/solution.py
+++ b/solution.py
@@ -61,6 +61,7 @@
         )
 
     chunks = [(a, h) for h in range(HALVES) for a in range(count)]
+    crossed = range(len(chunks) - len(chunks) // 4, len(chunks))
 
     def place(a, h, d):
         rows, cols = stepped[a].shape
@@ -134,8 +135,8 @@
         return remote(
             block,
             block,
-            c_send.at[(way + 1) // 2, c, owner // 2],
-            c_recv.at[c, owner // 2],
+            c_send.at[(way + 1) // 2, c, owner],
+            c_recv.at[c, owner],
             b + 2 * way if to is None else to,
         )
 
@@ -174,19 +175,28 @@
 
         cross_copy(c, b, b).start()
 
-    def line_finish(c, k):
+    def line_finish(c, k, shift):
         for way in (1, -1):
 
             @pl.when(has_source(way, k))
             def _():
-                owner = b - 2 * k * way
-                line_copy(c, owner, way, owner).wait_recv()
+                owner = b - 2 * k * way + shift
+                line_copy(c, owner, way, b - 2 * k * way).wait_recv()
 
                 @pl.when(has_next(way))
                 def _():
                     line_copy(c, owner, way).start()
 
-                cross_copy(c, owner, owner).start()
+                if c not in crossed:
+                    cross_copy(c, owner, owner).start()
+
+    def cross_arrive(c):
+        cross_copy(c, partner, partner).wait_recv()
+        for way in (1, -1):
+
+            @pl.when(has_next(way))
+            def _():
+                line_copy(c, partner, way).start()
 
     def vec_copy(k):
         to = lax.rem(b + k, n)
@@ -211,7 +221,7 @@
         pair_encode(c)
         pair_copy(c).start()
 
-    for t in range(len(chunks) + groups):
+    for t in range(len(chunks) + groups + 1):
         if t < len(chunks):
             pair_finish(t)
         if 0 <= t - 1 < len(chunks):
@@ -236,9 +246,13 @@
                 vec_back(k).start()
         for k in range(groups - 1, 0, -1):
             if 0 <= t - 1 - k < len(chunks):
-                line_finish(t - 1 - k, k)
-
-    for c in range(len(chunks)):
+                line_finish(t - 1 - k, k, 0)
+            if t - 2 - k in crossed:
+                line_finish(t - 2 - k, k, partner - b)
+        if t - 2 in crossed:
+            cross_arrive(t - 2)
+
+    for c in range(crossed.start):
         for k in range(groups):
             owner = 2 * other(k) + 1 - side
             cross_copy(c, owner, owner).wait_recv()
@@ -259,20 +273,21 @@
         for k in range(1, groups):
             to = other(k)
             part_copy(c, to, g, to).wait_send()
-        for k in range(groups):
+        for k in range(1 if c in crossed else groups):
             owner = 2 * other(k) + side
             cross_copy(c, owner, owner).wait_send()
-        for way in (1, -1):
-
-            @pl.when(has_next(way))
-            def _():
-                line_copy(c, b, way).wait_send()
-
-            for k in range(1, groups):
-
-                @pl.when(has_source(way, k) & has_next(way))
+        for shift in (0, partner - b) if c in crossed else (0,):
+            for way in (1, -1):
+
+                @pl.when(has_next(way))
                 def _():
-                    line_copy(c, b - 2 * k * way, way).wait_send()
+                    line_copy(c, b + shift, way).wait_send()
+
+                for k in range(1, groups):
+
+                    @pl.when(has_source(way, k) & has_next(way))
+                    def _():
+                        line_copy(c, b - 2 * k * way + shift, way).wait_send()
 
 
 def hand_over(count, *refs):
@@ -356,8 +371,8 @@
         + [dma((len(partials),))]
         + [dma((chunk_count,))] * 2
         + [dma((chunk_count, groups))] * 2
-        + [dma((2, chunk_count, groups))]
-        + [dma((chunk_count, groups))] * 3
+        + [dma((2, chunk_count, n)), dma((chunk_count, n))]
+        + [dma((chunk_count, groups))] * 2
         + [dma((n,))] * 4,
         compiler_params=pltpu.CompilerParams(collective_id=0, has_side_effects=True),
     )(

time: 66.9 us -> 69.5 us (1.039)
  Pallas kernels: 66 us -> 68.6 us
    pallas_call x1, Pallas kernels: 62 us -> 64.7 us  [per_device(): pl.pallas_call(functools.partial(kernel, n, kinds, limit), out_shape=out_...]
where the time goes in v3:
time: 69.5 us; the launch traced here: 69.3 us
  Pallas kernels  68.6 us (99%)
    pallas_call x1, Pallas kernels, per_device(): pl.pallas_call(functools.partial(kernel, n, kinds, limit), out_shape=out_...  64.7 us
    pallas_call x1, Pallas kernels, per_device(): pl.pallas_call(functools.partial(hand_over, len(large)), out_shape=tail_s...  3.95 us

profile of v3, /device:TPU:0, one launch (start us, length us, event | category | flops | bytes accessed | tf_op | source)
XLA Modules:
  0.0 69.3 jit_solution(2629822278259487043)
XLA Ops:
  0.6 64.7 %shard_map.211 = (bf16[1024,256]{1,0:T(8,128)(2,1)}, bf16[1024,256]{1,0:T(8,128)(2,1)}, bf16[1024,256]{1,0:T(8,128)(2,1)}, bf16[256,1024]{1,0:T(8,128)(2,1)}, f3...) custom-call(f32[1,1024,256]{2,1,0:T(8,128)} %refs_0_.1, ...), custom_call_target="tpu_custom_call" | custom-call | tf_op jit(solution)/shard_map/pallas_call | solution.py:362
  65.3 4.0 %shard_map.212 = (bf16[1024,256]{1,0:T(8,128)(2,1)}, bf16[1024,256]{1,0:T(8,128)(2,1)}, bf16[1024,256]{1,0:T(8,128)(2,1)}, bf16[256,1024]{1,0:T(8,128)(2,1)}, f3...) custom-call(bf16[1024,256]{1,0:T(8,128)(2,1)} %get-tuple-element.34., ...), custom_call_target="tpu_custom_call" | custom-call | tf_op jit(solution)/shard_map/pallas_call | solution.py:390
